TPU v7x, 32 devices: a whole 2x2x4 slice. The times are simulated.
32 devices in a mesh: dp: 2 (over x), seq: 16 (over z, y, core).
Axes of the slice: x: 2, y: 2, z: 4, core: 2. Of those that a mesh axis runs over, the one named last changes fastest.
Arguments:
- tiles: bfloat16 [2, 16, 32, 4, 1024], P('dp', None, 'seq'), may hold values from -6 to 6
- patch_index: int32 [2, 16, 32, 4], P('dp', None, 'seq'), may hold values from 0 to 127
- pos_table: bfloat16 [128, 1024], replicated, may hold values from -6 to 6
- depth_kernel: bfloat16 [2, 27, 1024], replicated, may hold values from -1.25 to 1.25
- enc_gain: bfloat16 [2, 1024], replicated, may hold values from 0.099609375 to 1.8984375
- point_weight: bfloat16 [2, 1024, 1024], replicated, may hold values from -0.1875 to 0.1875
- action_ids: int32 [2, 16], replicated, may hold values from 0 to 7
- w_in: bfloat16 [1024, 5120], P('seq', 'dp'), may hold values from -0.1875 to 0.1875
- action_table: bfloat16 [8, 5120], P(None, 'dp'), may hold values from -6 to 6
- dyn_gain: bfloat16 [5120], P('dp'), may hold values from 0.099609375 to 1.8984375
- w_query: bfloat16 [5120, 5120], P('seq', 'dp'), may hold values from -0.078125 to 0.078125
- w_keyval: bfloat16 [5120, 2, 1024], P('seq', None, 'dp'), may hold values from -0.078125 to 0.078125
- seq_order: int32 [4], replicated, may hold values from 0 to 3, each once
Outputs:
- attended: bfloat16 [2, 16, 32, 4, 5120], P(None, None, 'seq', None, 'dp')
Inputs may be any that keep to these rules, and one draw needn't show every extreme that they name: `seq_order`: each of 0 to 3 appears once.
All inputs are finite; a program needn't handle non-finite values.
Results may differ from a plain program's by a relative error of at most 0.012.
Values may be sent and summed in bfloat16 or wider, within the bound.
A program may use at most 128 MiB of HBM per device.

v0:
```python
import functools
import math

import jax
import jax.numpy as jnp
from jax import lax
from jax.experimental import pallas as pl
from jax.experimental.pallas import tpu as pltpu
from jax.sharding import PartitionSpec as P

DIM = 5120
HEAD = 128
Q_HEADS = 40
KV_HEADS = 8
MESH = pl.DeviceIdType.MESH


def gelu(z):
    return 0.5 * z * (1.0 + jnp.tanh(0.7978845608028654 * (z + 0.044715 * (z * z * z))))


def flipped(t, mask, bits):
    for bit in bits:
        if mask & bit:
            t = t + bit - 2 * bit * ((t // bit) % 2)
    return t


def window_kernel(
    sizes,
    pack_ref,
    in_ref,
    aux_ref,
    start_ref,
    taps_ref,
    gains_ref,
    point_ref,
    pick_ref,
    out_ref,
    w_all,
    in_all,
    aux_all,
    lat_all,
    embeds,
    squares,
    mixed,
    halos,
    middle,
    conv,
    latent_ref,
    h_send,
    h_recv,
    w_send,
    w_recv,
    i_send,
    i_recv,
    l_send,
    l_recv,
    a_send,
    a_recv,
    o_send,
    o_recv,
    own_sem,
):
    D, C, T, cells, kvg = sizes
    d = lax.axis_index("dp")
    seq = lax.axis_index("seq")
    c = seq // T
    t = seq % T
    bits = []
    bit = T // 2
    while bit:
        bits.append(bit)
        bit //= 2
    depth = pack_ref.shape[1]
    in_rows, in_cols = in_ref.shape
    tokens = latent_ref.shape[0]
    group = Q_HEADS // KV_HEADS
    qcols = kvg * group * HEAD

    def to_c(shift):
        return (d, ((c + shift) % C) * T + t)

    def to_t(bit):
        return (d, c * T + flipped(t, bit, bits))

    def to_d(shift):
        return ((d + shift) % D, seq)

    peers = [to_c(s) for s in range(1, C)] + [to_t(b) for b in bits] + [to_d(s) for s in range(1, D)]
    S = C * T
    above, below = (d, (seq + S - 1) % S), (d, (seq + 1) % S)
    peers += [above, below]
    barrier = pltpu.get_barrier_semaphore()
    for peer in peers:
        pl.semaphore_signal(barrier, inc=1, device_id=peer, device_id_type=MESH)
    pl.semaphore_wait(barrier, len(peers))

    sends = []

    def push(src, dst, send_sem, recv_sem, peer):
        copy = pltpu.make_async_remote_copy(
            src_ref=src,
            dst_ref=dst,
            send_sem=send_sem,
            recv_sem=recv_sem,
            device_id=peer,
            device_id_type=MESH,
        )
        copy.start()
        sends.append(copy)

    def arrived(ref, sem):
        pltpu.make_async_copy(ref, ref, sem).wait()

    def w_slot(s, m):
        origin = ((c + C - s) % C) * T + flipped(t, m, bits)
        return w_all.at[pl.ds(pl.multiple_of(origin * depth, depth), depth)]

    def i_slot(s, m, e):
        origin = ((c + C - s) % C) * T + flipped(t, m, bits)
        column = ((d + D - e) % D) * in_cols
        return in_all.at[
            pl.ds(pl.multiple_of(origin * in_rows, in_rows), in_rows),
            pl.ds(pl.multiple_of(column, HEAD), in_cols),
        ]

    def l_slot(s, e):
        row = ((d + D - e) % D) * tokens
        return lat_all.at[(c + C - s) % C, pl.ds(pl.multiple_of(row, tokens), tokens)]

    def a_slot(e):
        column = ((d + D - e) % D) * in_cols
        return aux_all.at[:, pl.ds(pl.multiple_of(column, HEAD), in_cols)]

    def w_forward(s, m, src):
        low = -1
        for b in bits:
            if m & b:
                low = bits.index(b)
        for index in range(low + 1, len(bits)):
            b = bits[index]
            push(src, w_slot(s, m), w_send.at[s, m | b], w_recv.at[s, m | b], to_t(b))

    early, last = bits[:-1], bits[-1]

    def i_forward(s, m, e, src):
        low = -1
        for b in early:
            if m & b:
                low = bits.index(b)
        if e == 0:
            for index in range(low + 1, len(early)):
                b = early[index]
                push(src, i_slot(s, m, e), i_send.at[s, m | b, e], i_recv.at[s, m | b, e], to_t(b))
            for shift in range(1, D):
                push(src, i_slot(s, m, e), i_send.at[s, m, shift], i_recv.at[s, m, shift], to_d(shift))
        push(src, i_slot(s, m, e), i_send.at[s, m | last, e], i_recv.at[s, m | last, e], to_t(last))

    def l_forward(s, src):
        for e in range(1, D):
            push(src, l_slot(s, 0), l_send.at[s, e], l_recv.at[s, e], to_d(e))

    own = [
        pltpu.make_async_copy(pack_ref.at[c], w_slot(0, 0), own_sem.at[0]),
        pltpu.make_async_copy(in_ref, i_slot(0, 0, 0), own_sem.at[1]),
        pltpu.make_async_copy(aux_ref, a_slot(0), own_sem.at[3]),
    ]
    for copy in own:
        copy.start()
    height, breadth, frames, channels = start_ref.shape

    def share_rows(l, source):
        push(source.at[height - 1], halos.at[l, 0], h_send.at[l, 0], h_recv.at[l, 0], below)
        push(source.at[0], halos.at[l, 1], h_send.at[l, 1], h_recv.at[l, 1], above)

    share_rows(0, start_ref)
    for shift in range(1, D):
        push(aux_ref, a_slot(0), a_send.at[shift], a_recv.at[shift], to_d(shift))
    for shift in range(1, C):
        push(in_ref, i_slot(0, 0, 0), i_send.at[shift, 0, 0], i_recv.at[shift, 0, 0], to_c(shift))
    i_forward(0, 0, 0, in_ref)
    for shift in range(1, C):
        push(
            pack_ref.at[(c + shift) % C],
            w_slot(0, 0),
            w_send.at[shift, 0],
            w_recv.at[shift, 0],
            to_c(shift),
        )
    w_forward(0, 0, pack_ref.at[c])

    def i_event(s, m, e):
        arrived(i_slot(s, m, e), i_recv.at[s, m, e])
        if not m & last:
            i_forward(s, m, e, i_slot(s, m, e))

    def w_event(s, m):
        arrived(w_slot(s, m), w_recv.at[s, m])
        w_forward(s, m, w_slot(s, m))

    def l_event(s, e):
        arrived(l_slot(s, e), l_recv.at[s, e])
        if e == 0:
            l_forward(s, l_slot(s, e))

    lanes = 256

    def encode(l, source):
        arrived(halos.at[l, 0], h_recv.at[l, 0])
        arrived(halos.at[l, 1], h_recv.at[l, 1])
        frame_ids = lax.broadcasted_iota(jnp.int32, (frames, lanes), 0)

        def lane_step(j, carry):
            cols = pl.ds(pl.multiple_of(j * lanes, lanes), lanes)
            taps = taps_ref[l, :, cols].astype(jnp.float32)

            def patch(r, w):
                if r < 0:
                    return jnp.where(seq > 0, halos[l, 0, w, :, cols].astype(jnp.float32), 0.0)
                if r == height:
                    return jnp.where(seq < S - 1, halos[l, 1, w, :, cols].astype(jnp.float32), 0.0)
                return source[r, w, :, cols].astype(jnp.float32)

            for r in range(height):
                for w in range(breadth):
                    sums = [None] * 3
                    for b in range(3):
                        for k in range(3):
                            if not 0 <= w + k - 1 < breadth:
                                continue
                            value = patch(r + b - 1, w + k - 1)
                            for a in range(3):
                                tap = 9 * a + 3 * b + k
                                term = value * taps[tap : tap + 1]
                                sums[a] = term if sums[a] is None else sums[a] + term
                    total = sums[2]
                    for a in range(2):
                        moved = pltpu.roll(sums[a], 2 - a, 0)
                        total = total + jnp.where(frame_ids >= 2 - a, moved, 0.0)
                    base = (r * breadth + w) * frames
                    conv[base : base + frames, cols] = total
            return carry

        lax.fori_loop(0, channels // lanes, lane_step, 0)
        summed = conv[...]
        factor = lax.rsqrt(jnp.mean(summed * summed, axis=-1, keepdims=True) + 1e-05)
        gain = gains_ref[l].astype(jnp.float32)
        normed = (summed * factor * gain[None]).astype(jnp.bfloat16)
        projected = jnp.dot(normed, point_ref[l], preferred_element_type=jnp.float32)
        change = gelu(projected)
        for r in range(height):
            for w in range(breadth):
                base = (r * breadth + w) * frames
                value = source[r, w].astype(jnp.float32) + change[base : base + frames]
                value = value.astype(jnp.bfloat16)
                if l + 1 < point_ref.shape[0]:
                    middle[l, r, w] = value
                else:
                    latent_ref[base : base + frames] = value

    source = start_ref
    for l in range(point_ref.shape[0]):
        encode(l, source)
        if l + 1 < point_ref.shape[0]:
            source = middle.at[l]
            share_rows(l + 1, source)
            for s in range(1, C):
                i_event(s, 0, 0)
    for shift in range(1, C):
        push(latent_ref, l_slot(0, 0), l_send.at[shift, 0], l_recv.at[shift, 0], to_c(shift))
    l_forward(0, latent_ref)
    latent_copy = pltpu.make_async_copy(latent_ref, l_slot(0, 0), own_sem.at[2])
    latent_copy.start()
    own.append(latent_copy)

    order_w = sorted(
        ((m.bit_count(), s, m) for s in range(C) for m in range(T) if s or m),
        key=lambda item: (item[0] + item[1], item[0]),
    )
    w_todo = [(s, m) for _, s, m in order_w]
    for m in sorted((m for m in range(1, T) if not m & last), key=lambda m: m.bit_count()):
        for s in range(C):
            i_event(s, m, 0)
    for s in range(1, C):
        l_event(s, 0)
    for e in range(1, D):
        arrived(a_slot(e), a_recv.at[e])
        for m in range(T):
            if not m & last:
                for s in range(C):
                    i_event(s, m, e)
    for s, m in list(w_todo):
        if m == 0:
            w_event(s, m)
            w_todo.remove((s, m))
    for m in range(T):
        if m & last:
            for e in range(D):
                for s in range(C):
                    i_event(s, m, e)
    for e in range(1, D):
        for s in range(C):
            l_event(s, e)
    for copy in own:
        copy.wait()

    chunk = 512
    rows = D * tokens

    def embed_block(shift):
        where = (c + shift) % C
        squares[where] = jnp.zeros((rows, HEAD), jnp.float32)

        def step(j, carry):
            cols = pl.ds(pl.multiple_of(j * chunk, chunk), chunk)
            z = jnp.dot(lat_all[where], in_all[:, cols], preferred_element_type=jnp.float32)
            z = z + jnp.dot(pick_ref[...], aux_all[:, cols], preferred_element_type=jnp.float32)
            g = gelu(z)
            gain = aux_all[:, cols].astype(jnp.float32)[8:9]
            embeds[where, :, cols] = (g * gain).astype(jnp.bfloat16)
            square = g * g
            part = square[:, :HEAD]
            for k in range(1, chunk // HEAD):
                part = part + square[:, k * HEAD : (k + 1) * HEAD]
            squares[where] += part
            return carry

        lax.fori_loop(0, embeds.shape[2] // chunk, step, 0)

    per = -(-len(w_todo) // C)
    for shift in range(C):
        embed_block(shift)
        for s, m in w_todo[shift * per : (shift + 1) * per]:
            w_event(s, m)

    row_ids = lax.broadcasted_iota(jnp.int32, (tokens, tokens), 0)
    col_ids = lax.broadcasted_iota(jnp.int32, (tokens, tokens), 1)
    seen = (row_ids // frames == col_ids // frames) & (row_ids >= col_ids)

    def unit(x):
        return x * lax.rsqrt(jnp.mean(x * x, axis=-1, keepdims=True) + 1e-06)

    def mix_block(where):
        total = jnp.dot(embeds[where], w_all[...], preferred_element_type=jnp.float32)
        mean = jnp.sum(squares[where], axis=-1, keepdims=True) / DIM
        total = total * lax.rsqrt(mean + 1e-05)
        for kv in range(kvg):
            at = qcols + kv * HEAD
            key = unit(total[:, at : at + HEAD]).astype(jnp.bfloat16)
            at = qcols + (kvg + kv) * HEAD
            value = total[:, at : at + HEAD].astype(jnp.bfloat16)
            for h in range(kv * group, (kv + 1) * group):
                query = unit(total[:, h * HEAD : (h + 1) * HEAD]) * HEAD**-0.5
                query = query.astype(jnp.bfloat16)
                for clip in range(D):
                    span = slice(clip * tokens, (clip + 1) * tokens)
                    score = lax.dot_general(
                        query[span],
                        key[span],
                        (((1,), (1,)), ((), ())),
                        preferred_element_type=jnp.float32,
                    )
                    raised = jnp.where(seen, jnp.exp(score), 0.0)
                    shares = raised / jnp.sum(raised, axis=-1, keepdims=True)
                    result = jnp.dot(
                        shares.astype(jnp.bfloat16), value[span], preferred_element_type=jnp.float32
                    )
                    mixed[where, span, h * HEAD : (h + 1) * HEAD] = result.astype(jnp.bfloat16)

    mine = pl.ds(pl.multiple_of(c * qcols, HEAD), qcols)

    def send_of(shift):
        where = (c + shift) % C
        return pltpu.make_async_remote_copy(
            src_ref=mixed.at[where],
            dst_ref=out_ref.at[:, mine],
            send_sem=o_send.at[shift],
            recv_sem=o_recv.at[shift],
            device_id=(d, where * T + t),
            device_id_type=MESH,
        )

    def mix_step(index, carry):
        shift = index + 1
        mix_block((c + shift) % C)
        send_of(shift).start()
        return carry

    lax.fori_loop(0, C - 1, mix_step, 0)
    mix_block(c)
    keep = pltpu.make_async_copy(mixed.at[c], out_ref.at[:, mine], own_sem.at[0])
    keep.start()
    for shift in range(1, C):
        send_of(shift).wait_send()
        column = ((c + C - shift) % C) * qcols
        arrived(out_ref.at[:, pl.ds(pl.multiple_of(column, HEAD), qcols)], o_recv.at[shift])
    keep.wait()
    for copy in sends:
        copy.wait_send()


def body(
    tiles,
    patch_index,
    pos_table,
    depth_kernel,
    enc_gain,
    point_weight,
    action_ids,
    w_in,
    action_table,
    dyn_gain,
    w_query,
    w_keyval,
    seq_order,
):
    clip_local, frames, height, breadth, channels = tiles.shape
    positions = pos_table.shape[0]
    blocks = depth_kernel.shape[0]
    D, S = lax.axis_size("dp"), lax.axis_size("seq")
    kv_local = w_keyval.shape[2] // HEAD
    C = math.gcd(kv_local, S)
    T = S // C
    assert T & (T - 1) == 0 and T > 1 and clip_local == 1
    kvg = kv_local // C
    group = Q_HEADS // KV_HEADS
    depth = w_query.shape[0]
    frames_first = (0, 3, 1, 2, 4)

    flat_index = patch_index.reshape(-1)
    position_pick = (flat_index[:, None] == jnp.arange(positions, dtype=jnp.int32)[None, :]).astype(
        jnp.bfloat16
    )
    placed = jnp.dot(position_pick, pos_table, preferred_element_type=jnp.float32).reshape(
        tiles.shape
    )
    hidden = (tiles.astype(jnp.float32) + placed).astype(jnp.bfloat16)
    start = hidden[0].transpose(1, 2, 0, 3)

    cells = height * breadth
    tokens = frames * cells
    pack = jnp.concatenate(
        [
            w_query.reshape(depth, C, -1).transpose(1, 0, 2),
            w_keyval.reshape(depth, 2, C, -1).transpose(2, 0, 1, 3).reshape(C, depth, -1),
        ],
        axis=2,
    )
    actions = action_table.shape[0]
    assert actions == 8
    aux = jnp.concatenate(
        [action_table, dyn_gain[None], jnp.zeros((7, action_table.shape[1]), jnp.bfloat16)], axis=0
    )
    pick = (
        jnp.tile(action_ids[:, None, :], (1, cells, 1)).reshape(-1)[:, None] == jnp.arange(16, dtype=jnp.int32)[None]
    ).astype(jnp.bfloat16)
    width = pack.shape[2]
    qcols = kvg * group * HEAD
    bf16, f32 = jnp.bfloat16, jnp.float32
    dma = pltpu.SemaphoreType.DMA
    out = pl.pallas_call(
        functools.partial(window_kernel, (D, C, T, cells, kvg)),
        out_shape=jax.ShapeDtypeStruct((D * tokens, C * qcols), bf16),
        in_specs=[pl.BlockSpec(memory_space=pltpu.VMEM)] * 8,
        out_specs=pl.BlockSpec(memory_space=pltpu.VMEM),
        scratch_shapes=[
            pltpu.VMEM((S * depth, width), bf16),
            pltpu.VMEM((channels, DIM), bf16),
            pltpu.VMEM((16, DIM), bf16),
            pltpu.VMEM((C, D * tokens, channels), bf16),
            pltpu.VMEM((C, D * tokens, DIM), bf16),
            pltpu.VMEM((C, D * tokens, HEAD), f32),
            pltpu.VMEM((C, D * tokens, qcols), bf16),
            pltpu.VMEM((blocks, 2, breadth, frames, channels), bf16),
            pltpu.VMEM((max(blocks - 1, 1), height, breadth, frames, channels), bf16),
            pltpu.VMEM((tokens, channels), f32),
            pltpu.VMEM((tokens, channels), bf16),
            dma((blocks, 2)),
            dma((blocks, 2)),
            dma((C, T)),
            dma((C, T)),
            dma((C, T, D)),
            dma((C, T, D)),
            dma((C, D)),
            dma((C, D)),
            dma((D,)),
            dma((D,)),
            dma((C,)),
            dma((C,)),
            dma((4,)),
        ],
        compiler_params=pltpu.CompilerParams(
            collective_id=0, has_side_effects=True, vmem_limit_bytes=60 * 1024 * 1024
        ),
    )(pack, w_in, aux, start, depth_kernel, enc_gain, point_weight, pick)
    out = out.reshape(D, height, breadth, frames, -1).transpose(frames_first)
    return jnp.take(out, seq_order, axis=3)


def solution(mesh):
    placed = (
        P("dp", None, "seq", None, None),
        P("dp", None, "seq", None),
        P(),
        P(),
        P(),
        P(),
        P(),
        P("seq", "dp"),
        P(None, "dp"),
        P("dp"),
        P("seq", "dp"),
        P("seq", None, "dp"),
        P(),
    )
    return jax.shard_map(
        body,
        mesh=mesh,
        in_specs=placed,
        out_specs=P(None, None, "seq", None, "dp"),
        check_vma=False,
    )
```

profile of v0, /device:TPU:11, one launch (start us, length us, event | category | flops | bytes accessed | tf_op | source)
XLA Modules:
  0.0 209.0 jit_solution(16619851046340161356)
XLA Ops:
  0.0 0.0 copy-start
  0.0 1.6 copy.35
  1.6 0.0 copy-done
  1.7 1.3 bitcast_bitcast_fusion.1
  2.9 2.2 %reshape.29 = bf16[4,320,256]{2,1,0:T(8,128)(2,1)S(1)} reshape(bf16[4,320,2,128]{3,2,1,0:T(2,128)(2,1)} %bitcast_bitcast_fusion.1) | data formatting | bytes 1310720 | tf_op jit(solution)/shard_map/reshape | solution.py:446
  5.2 0.0 copy-start.6
  5.2 0.0 copy-start.1
  5.2 1.6 pad_maximum_fusion.pack_ref
  6.8 0.0 copy-done.6
  6.8 0.0 copy-start.4
  6.8 0.1 copy.21
  6.9 0.1 eq.28
  7.0 0.0 copy-done.1
  7.1 0.0 copy-start.7
  7.1 0.3 fusion.3
  7.3 0.1 reshape.30
  7.5 0.3 copy-done.2
  7.8 1.1 fusion.1.start_ref
  8.9 0.0 copy-done.3
  8.9 0.7 copy.23.taps_ref
  9.6 0.0 copy-done.5
  9.6 0.1 pad.2.clone
  9.7 0.0 copy-done.4
  9.7 0.7 maximum_maximum_fusion.aux_ref
  10.4 0.0 copy-done.7
  10.4 0.1 tile.8
  10.5 0.7 fusion.2.pick_ref
  11.2 193.5 %shard_map.127 = bf16[256,2560]{1,0:T(8,128)(2,1)} custom-call(bf16[4,320,896]{2,1,0:T(8,128)(2,1)} %pad_maximum_fusion.pack_ref, bf16[64,2560]{1,0:T(8,128)(2,1)} %in_ref.1, bf16[16,2560]{1,0:T(8,128)(2,1)} %maximum_maximum_fusion.aux_ref, bf16[2,4,16,1024]{3,2,1,0:T(8,128)(2,1)} %fusion.1.start_ref, bf16[2,27,1024]{2,1,0:T(8,128)(2,1)} %copy.23.taps_ref, ...), custom_call_target="tpu_custom_call" | custom-call | tf_op jit(solution)/shard_map/pallas_call | solution.py:462
  204.7 0.0 copy-done.8
  204.8 1.9 gather_fusion
  206.8 0.2 select_bitcast_fusion
  206.9 2.1 copy.24
  (10 shorter events, 0.1 us)
Async XLA Ops:
  0.0 1.6 copy-start
  5.2 1.6 copy-start.6
  5.2 1.9 copy-start.1
  6.8 1.0 copy-start.2
  6.8 2.1 copy-start.3
  6.8 2.8 %copy-start.5 = (bf16[2560]{0:T(1024)(128)(2,1)S(1)}, bf16[2560]{0:T(1024)(128)(2,1)}, u32[]{:S(2)}) copy-start(bf16[2560]{0:T(1024)(128)(2,1)} %param.22) | copy-start | bytes 15364
  6.8 2.9 %copy-start.4 = (bf16[8,2560]{1,0:T(8,128)(2,1)S(1)}, bf16[8,2560]{1,0:T(8,128)(2,1)}, u32[]{:S(2)}) copy-start(bf16[8,2560]{1,0:T(8,128)(2,1)} %param.21) | copy-start | bytes 122884
  7.1 3.3 %copy-start.7 = (s32[2,16]{1,0:T(2,128)S(1)}, s32[2,16]{1,0:T(2,128)}, u32[]{:S(2)}) copy-start(s32[2,16]{1,0:T(2,128)} %param.19) | copy-start | bytes 388
  11.2 193.5 %copy-start.8 = (s32[4]{0:T(128)S(1)}, s32[4]{0:T(128)}, u32[]{:S(2)}) copy-start(s32[4]{0:T(128)} %param.25) | copy-start | bytes 52
where the time goes:
time: 210 us; the launch traced here: 209 us
  Pallas kernels  194 us (92%)
  local copies, waits for them, and re-layouts  10.7 us (5%)
  other arithmetic  4.38 us (2%)
    pallas_call x1, Pallas kernels, body(): pl.pallas_call(functools.partial(window_kernel, (D, C, T, cells, kvg)), o...  194 us

commit v1 on v0

v1 whole, which is shorter than its diff:
```python
import functools
import math

import jax
import jax.numpy as jnp
from jax import lax
from jax.experimental import pallas as pl
from jax.experimental.pallas import tpu as pltpu
from jax.sharding import PartitionSpec as P

DIM = 5120
HEAD = 128
Q_HEADS = 40
KV_HEADS = 8
MESH = pl.DeviceIdType.MESH


def gelu(z):
    return 0.5 * z * (1.0 + jnp.tanh(0.7978845608028654 * (z + 0.044715 * (z * z * z))))


def flipped(t, mask, bits):
    for bit in bits:
        if mask & bit:
            t = t + bit - 2 * bit * ((t // bit) % 2)
    return t


def window_kernel(
    sizes,
    pack_ref,
    in_ref,
    aux_ref,
    start_ref,
    taps_ref,
    gains_ref,
    point_ref,
    pick_ref,
    out_ref,
    w_all,
    in_all,
    aux_all,
    lat_all,
    embeds,
    squares,
    mixed,
    keys,
    values,
    halos,
    middle,
    conv,
    latent_ref,
    h_send,
    h_recv,
    w_send,
    w_recv,
    i_send,
    i_recv,
    l_send,
    l_recv,
    a_send,
    a_recv,
    o_send,
    o_recv,
    own_sem,
    zi_send,
    zl_send,
):
    D, C, T, edge = sizes
    d = lax.axis_index("dp")
    seq = lax.axis_index("seq")
    c = seq // T
    t = seq % T
    bits = []
    bit = T // 2
    while bit:
        bits.append(bit)
        bit //= 2
    early, last = bits[:-1], bits[-1]
    near_masks = [m for m in range(T) if not m & last]
    near_masks.sort(key=lambda m: m.bit_count())
    depth = pack_ref.shape[1]
    in_rows, in_cols = in_ref.shape
    tokens = latent_ref.shape[0]
    group = Q_HEADS // KV_HEADS
    qcols = group * HEAD

    orders = [
        sorted(range(C), key=lambda o, i=i: (abs(o - i), o if 2 * i < C else -o)) for i in range(C)
    ]

    def nearest(h):
        value = orders[0][h]
        for i in range(1, C):
            value = jnp.where(c == i, orders[i][h], value)
        return value

    origins = [c] + [nearest(h) for h in range(1, C)]

    def to_c(shift):
        return (d, ((c + shift) % C) * T + t)

    def to_t(bit):
        return (d, c * T + flipped(t, bit, bits))

    def to_d(shift):
        return ((d + shift) % D, seq)

    peers = [to_c(s) for s in range(1, C)] + [to_t(b) for b in bits] + [to_d(s) for s in range(1, D)]
    S = C * T
    above, below = (d, (seq + S - 1) % S), (d, (seq + 1) % S)
    peers += [above, below]
    with jax.named_scope("barrier"):
        barrier = pltpu.get_barrier_semaphore()
        for peer in peers:
            pl.semaphore_signal(barrier, inc=1, device_id=peer, device_id_type=MESH)
        pl.semaphore_wait(barrier, len(peers))

    sends = []

    def push(src, dst, send_sem, recv_sem, peer, guard=None):
        copy = pltpu.make_async_remote_copy(
            src_ref=src,
            dst_ref=dst,
            send_sem=send_sem,
            recv_sem=recv_sem,
            device_id=peer,
            device_id_type=MESH,
        )
        if guard is None:
            copy.start()
        else:
            pl.when(guard)(copy.start)
        sends.append((copy, guard))

    def arrived(ref, sem):
        pltpu.make_async_copy(ref, ref, sem).wait()

    w_cols = ((0, edge), (edge, pack_ref.shape[2] - edge))
    pieces = [(g, r) for g in range(2) for r in range(2)]

    def w_slot(o, m, piece):
        g, r = piece
        origin = o * T + flipped(t, m, bits)
        return w_all.at[
            pl.ds(pl.multiple_of(origin * depth + r * (depth // 2), depth // 2), depth // 2),
            pl.ds(*w_cols[g]),
        ]

    def w_own(target, piece):
        g, r = piece
        return pack_ref.at[target, pl.ds(r * (depth // 2), depth // 2), pl.ds(*w_cols[g])]

    split = in_rows * 3 // 4
    WHOLE, HEAD_PART, TAIL_PART = 0, 1, 2

    def part_rows(part):
        return ((0, in_rows), (0, split), (split, in_rows - split))[part]

    def i_slot(o, m, e, part):
        first, count = part_rows(part)
        origin = o * T + flipped(t, m, bits)
        column = ((d + D - e) % D) * in_cols
        return in_all.at[
            pl.ds(pl.multiple_of(origin * in_rows + first, math.gcd(in_rows, split)), count),
            pl.ds(pl.multiple_of(column, HEAD), in_cols),
        ]

    def l_slot(o, e):
        row = ((d + D - e) % D) * tokens
        return lat_all.at[o, pl.ds(pl.multiple_of(row, tokens), tokens)]

    def a_slot(e):
        column = ((d + D - e) % D) * in_cols
        return aux_all.at[:, pl.ds(pl.multiple_of(column, HEAD), in_cols)]

    def along(o):
        ahead = jnp.where(o < c, 1, -1)
        target = c + ahead
        guard = (target >= 0) & (target < C)
        return (d, jnp.clip(target, 0, C - 1) * T + t), guard

    def below_above(src, dst, send_sems, recv_sem):
        if C == 1:
            return
        push(src, dst, send_sems.at[0], recv_sem, (d, jnp.minimum(c + 1, C - 1) * T + t), c + 1 < C)
        push(src, dst, send_sems.at[1], recv_sem, (d, jnp.maximum(c - 1, 0) * T + t), c >= 1)

    def w_forward(o, m, piece, src):
        k = pieces.index(piece)
        low = -1
        for b in bits:
            if m & b:
                low = bits.index(b)
        for b in bits[low + 1 :]:
            push(src, w_slot(o, m, piece), w_send.at[o, m | b, k], w_recv.at[o, m | b, k], to_t(b))

    def w_across(h, piece):
        k = pieces.index(piece)
        target = origins[h]
        push(
            w_own(target, piece),
            w_slot(c, 0, piece),
            w_send.at[target, 0, k],
            w_recv.at[c, 0, k],
            (d, target * T + t),
        )

    def i_push(o, m, e, part, own, new_m, new_e, peer):
        first, count = part_rows(part)
        src = in_ref.at[pl.ds(first, count)] if own else i_slot(o, m, e, part)
        k = int(part == TAIL_PART)
        push(src, i_slot(o, m, e, part), i_send.at[o, new_m, new_e, k], i_recv.at[o, new_m, new_e, k], peer)

    def i_forward(o, m, e, part, own=False):
        if m & last:
            return
        low = -1
        for b in early:
            if m & b:
                low = early.index(b)
        later = early[low + 1 :]
        if e == 0:
            for b in later:
                i_push(o, m, e, WHOLE, own, m | b, e, to_t(b))
            for shift in range(1, D):
                i_push(o, m, e, HEAD_PART if m else WHOLE, own, m, shift, to_d(shift))
        elif m == 0 or part == TAIL_PART:
            for b in later:
                i_push(o, m, e, TAIL_PART, own, m | b, e, to_t(b))
        i_push(o, m, e, part, own, m | last, e, to_t(last))

    def l_forward(o, src):
        for e in range(1, D):
            push(src, l_slot(o, 0), l_send.at[o, e], l_recv.at[o, e], to_d(e))

    own = [
        pltpu.make_async_copy(
            pack_ref.at[c], w_all.at[pl.ds(pl.multiple_of(seq * depth, depth), depth)], own_sem.at[0]
        ),
        pltpu.make_async_copy(in_ref, i_slot(c, 0, 0, WHOLE), own_sem.at[1]),
        pltpu.make_async_copy(aux_ref, a_slot(0), own_sem.at[3]),
    ]
    for copy in own:
        copy.start()
    height, breadth, frames, channels = start_ref.shape

    def share_rows(l, source):
        push(source.at[height - 1], halos.at[l, 0], h_send.at[l, 0], h_recv.at[l, 0], below)
        push(source.at[0], halos.at[l, 1], h_send.at[l, 1], h_recv.at[l, 1], above)

    share_rows(0, start_ref)
    below_above(in_ref, i_slot(c, 0, 0, WHOLE), zi_send, i_recv.at[c, 0, 0, 0])
    i_forward(c, 0, 0, WHOLE, own=True)
    for shift in range(1, D):
        push(aux_ref, a_slot(0), a_send.at[shift], a_recv.at[shift], to_d(shift))

    def i_event(o, m, e, part=0):
        arrived(i_slot(o, m, e, part), i_recv.at[o, m, e, int(part == TAIL_PART)])
        i_forward(o, m, e, part)

    def iz_event(h):
        o = origins[h]
        slot = i_slot(o, 0, 0, WHOLE)
        arrived(slot, i_recv.at[o, 0, 0, 0])
        peer, guard = along(o)
        push(slot, slot, zi_send.at[1 + h], i_recv.at[o, 0, 0, 0], peer, guard)
        i_forward(o, 0, 0, WHOLE)

    def w_event(h, m, piece):
        o = origins[h]
        slot = w_slot(o, m, piece)
        arrived(slot, w_recv.at[o, m, pieces.index(piece)])
        w_forward(o, m, piece, slot)

    w_pushes = []
    for piece in pieces:
        w_pushes += [(h, piece) for h in range(C - 1, -1, -1)]

    def w_start(count):
        for h, piece in w_pushes[:count]:
            if h:
                w_across(h, piece)
            else:
                w_forward(c, 0, piece, w_own(c, piece))
        del w_pushes[:count]

    def lz_event(h):
        o = origins[h]
        slot = l_slot(o, 0)
        arrived(slot, l_recv.at[o, 0])
        peer, guard = along(o)
        push(slot, slot, zl_send.at[1 + h], l_recv.at[o, 0], peer, guard)
        l_forward(o, slot)

    lanes = 256

    def encode(l, source):
        arrived(halos.at[l, 0], h_recv.at[l, 0])
        arrived(halos.at[l, 1], h_recv.at[l, 1])
        frame_ids = lax.broadcasted_iota(jnp.int32, (frames, lanes), 0)

        def lane_step(j, carry):
            cols = pl.ds(pl.multiple_of(j * lanes, lanes), lanes)
            taps = taps_ref[l, :, cols].astype(jnp.float32)

            def patch(r, w):
                if r < 0:
                    return jnp.where(seq > 0, halos[l, 0, w, :, cols].astype(jnp.float32), 0.0)
                if r == height:
                    return jnp.where(seq < S - 1, halos[l, 1, w, :, cols].astype(jnp.float32), 0.0)
                return source[r, w, :, cols].astype(jnp.float32)

            for r in range(height):
                for w in range(breadth):
                    sums = [None] * 3
                    for b in range(3):
                        for k in range(3):
                            if not 0 <= w + k - 1 < breadth:
                                continue
                            value = patch(r + b - 1, w + k - 1)
                            for a in range(3):
                                tap = 9 * a + 3 * b + k
                                term = value * taps[tap : tap + 1]
                                sums[a] = term if sums[a] is None else sums[a] + term
                    total = sums[2]
                    for a in range(2):
                        moved = pltpu.roll(sums[a], 2 - a, 0)
                        total = total + jnp.where(frame_ids >= 2 - a, moved, 0.0)
                    base = (r * breadth + w) * frames
                    conv[base : base + frames, cols] = total
            return carry

        lax.fori_loop(0, channels // lanes, lane_step, 0)
        summed = conv[...]
        factor = lax.rsqrt(jnp.mean(summed * summed, axis=-1, keepdims=True) + 1e-05)
        gain = gains_ref[l].astype(jnp.float32)
        normed = (summed * factor * gain[None]).astype(jnp.bfloat16)
        projected = jnp.dot(normed, point_ref[l], preferred_element_type=jnp.float32)
        change = gelu(projected)
        for r in range(height):
            for w in range(breadth):
                base = (r * breadth + w) * frames
                value = source[r, w].astype(jnp.float32) + change[base : base + frames]
                value = value.astype(jnp.bfloat16)
                if l + 1 < point_ref.shape[0]:
                    middle[l, r, w] = value
                else:
                    latent_ref[base : base + frames] = value

    def local_events(h):
        o = origins[h]
        for m in near_masks:
            if m:
                i_event(o, m, 0)
        for e in range(1, D):
            i_event(o, 0, e)

    source = start_ref
    for l in range(point_ref.shape[0]):
        with jax.named_scope("encode"):
            encode(l, source)
        if l + 1 < point_ref.shape[0]:
            source = middle.at[l]
            share_rows(l + 1, source)
            w_start(1)
            if l == 0 and C > 1:
                with jax.named_scope("iz1"):
                    iz_event(1)
    below_above(latent_ref, l_slot(c, 0), zl_send, l_recv.at[c, 0])
    l_forward(c, latent_ref)
    latent_copy = pltpu.make_async_copy(latent_ref, l_slot(c, 0), own_sem.at[2])
    latent_copy.start()
    own.append(latent_copy)

    def local_events(h):
        o = origins[h]
        with jax.named_scope("local%d" % h):
            for m in near_masks:
                if m:
                    i_event(o, m, 0)
            for e in range(1, D):
                i_event(o, 0, e)

    def w_events(piece, count):
        with jax.named_scope("w%d_%d" % (pieces.index(piece), count)):
            for m in range(T):
                if (m & ~last).bit_count() + (T if m & last else 0) == count:
                    for h in range(C - 1, -1, -1):
                        if h or m:
                            w_event(h, m, piece)

    w_start(1)
    local_events(0)
    for h in range(1, C):
        if h > 1:
            with jax.named_scope("iz%d" % h):
                iz_event(h)
            w_start(1)
        with jax.named_scope("lz%d" % h):
            lz_event(h)
        local_events(h)
    w_start(len(w_pushes))
    steps = len(early) + 1
    w_todo = []
    for k in range(len(pieces) + steps - 1):
        for count in range(steps):
            if 0 <= k - count < len(pieces):
                w_todo.append((pieces[k - count], count))

    def core_events(e):
        with jax.named_scope("core"):
            for h in range(C):
                for m in near_masks:
                    if m and e:
                        i_event(origins[h], m | last, e, HEAD_PART)
                        i_event(origins[h], m | last, e, TAIL_PART)
                    else:
                        i_event(origins[h], m | last, e)

    def cross_events(e):
        with jax.named_scope("cross"):
            for h in range(C):
                for m in near_masks:
                    if m:
                        i_event(origins[h], m, e, HEAD_PART)
                        i_event(origins[h], m, e, TAIL_PART)

    chunk = math.gcd(in_cols, 512)
    rows = D * tokens

    def embed_block(where, e):
        first = ((d + D - e) % D) * in_cols
        if e == 0:
            squares[where] = jnp.zeros((rows, HEAD), jnp.float32)

        def step(j, carry):
            cols = pl.ds(pl.multiple_of(first + j * chunk, HEAD), chunk)
            z = jnp.dot(lat_all[where], in_all[:, cols], preferred_element_type=jnp.float32)
            z = z + jnp.dot(pick_ref[...], aux_all[:, cols], preferred_element_type=jnp.float32)
            g = gelu(z)
            gain = aux_all[:, cols].astype(jnp.float32)[8:9]
            embeds[where, :, cols] = (g * gain).astype(jnp.bfloat16)
            square = g * g
            part = square[:, :HEAD]
            for k in range(1, chunk // HEAD):
                part = part + square[:, k * HEAD : (k + 1) * HEAD]
            squares[where] += part
            return carry

        with jax.named_scope("embed"):
            lax.fori_loop(0, in_cols // chunk, step, 0)

    if w_todo:
        w_events(*w_todo.pop(0))
    core_events(0)
    for copy in own:
        copy.wait()
    per = -(-(len(w_todo)) // (C * D))
    for e in range(D):
        if e:
            cross_events(e)
            with jax.named_scope("aux"):
                arrived(a_slot(e), a_recv.at[e])
            core_events(e)
        for h in range(C):
            if e == 0:
                with jax.named_scope("lx%d" % h):
                    for k in range(1, D):
                        arrived(l_slot(origins[h], k), l_recv.at[origins[h], k])
            embed_block(origins[h], e)
            for item in w_todo[:per]:
                w_events(*item)
            del w_todo[:per]

    row_ids = lax.broadcasted_iota(jnp.int32, (tokens, tokens), 0)
    col_ids = lax.broadcasted_iota(jnp.int32, (tokens, tokens), 1)
    seen = (row_ids // frames == col_ids // frames) & (row_ids >= col_ids)

    def unit(x):
        return x * lax.rsqrt(jnp.mean(x * x, axis=-1, keepdims=True) + 1e-06)

    def mix_block(where, g):
        first, count = w_cols[g]
        total = jnp.dot(
            embeds[where], w_all[:, first : first + count], preferred_element_type=jnp.float32
        )
        mean = jnp.sum(squares[where], axis=-1, keepdims=True) / DIM
        total = total * lax.rsqrt(mean + 1e-05)
        if g == 0:
            keys[where] = unit(total[:, :HEAD]).astype(jnp.bfloat16)
            values[where] = total[:, HEAD : 2 * HEAD].astype(jnp.bfloat16)
        key, value = keys[where], values[where]
        for at in range(2 * HEAD if g == 0 else 0, count, HEAD):
            query = (unit(total[:, at : at + HEAD]) * HEAD**-0.5).astype(jnp.bfloat16)
            to = first + at - 2 * HEAD
            for clip in range(D):
                span = slice(clip * tokens, (clip + 1) * tokens)
                score = lax.dot_general(
                    query[span],
                    key[span],
                    (((1,), (1,)), ((), ())),
                    preferred_element_type=jnp.float32,
                )
                raised = jnp.where(seen, jnp.exp(score), 0.0)
                shares = raised / jnp.sum(raised, axis=-1, keepdims=True)
                result = jnp.dot(
                    shares.astype(jnp.bfloat16), value[span], preferred_element_type=jnp.float32
                )
                mixed[where, span, to : to + HEAD] = result.astype(jnp.bfloat16)

    def out_cols(g):
        first, count = w_cols[g]
        return (0, count - 2 * HEAD) if g == 0 else (first - 2 * HEAD, count)

    def send_of(where, g):
        first, count = out_cols(g)
        return pltpu.make_async_remote_copy(
            src_ref=mixed.at[where, :, pl.ds(first, count)],
            dst_ref=out_ref.at[:, pl.ds(pl.multiple_of(c * qcols + first, HEAD), count)],
            send_sem=o_send.at[where, g],
            recv_sem=o_recv.at[c, g],
            device_id=(d, where * T + t),
            device_id_type=MESH,
        )

    for g in range(2):
        for piece in pieces:
            if piece[0] == g:
                for count in range(T, T + steps):
                    w_events(piece, count)
        for h in range(C - 1, 0, -1):
            with jax.named_scope("mix"):
                mix_block(origins[h], g)
            send_of(origins[h], g).start()
    for g in range(2):
        with jax.named_scope("mix"):
            mix_block(c, g)
    keep = pltpu.make_async_copy(
        mixed.at[c], out_ref.at[:, pl.ds(pl.multiple_of(c * qcols, HEAD), qcols)], own_sem.at[0]
    )
    keep.start()
    with jax.named_scope("tail"):
        for g in range(2):
            first, count = out_cols(g)
            for h in range(C - 1, 0, -1):
                send_of(origins[h], g).wait_send()
                column = origins[h] * qcols + first
                arrived(
                    out_ref.at[:, pl.ds(pl.multiple_of(column, HEAD), count)], o_recv.at[origins[h], g]
                )
        keep.wait()
    for copy, guard in sends:
        if guard is None:
            copy.wait_send()
        else:
            pl.when(guard)(copy.wait_send)


def body(
    tiles,
    patch_index,
    pos_table,
    depth_kernel,
    enc_gain,
    point_weight,
    action_ids,
    w_in,
    action_table,
    dyn_gain,
    w_query,
    w_keyval,
    seq_order,
):
    clip_local, frames, height, breadth, channels = tiles.shape
    positions = pos_table.shape[0]
    blocks = depth_kernel.shape[0]
    D, S = lax.axis_size("dp"), lax.axis_size("seq")
    kv_local = w_keyval.shape[2] // HEAD
    C = math.gcd(kv_local, S)
    T = S // C
    assert T & (T - 1) == 0 and T > 1 and clip_local == 1 and kv_local == C
    group = Q_HEADS // KV_HEADS
    depth = w_query.shape[0]
    frames_first = (0, 3, 1, 2, 4)

    flat_index = patch_index.reshape(-1)
    position_pick = (flat_index[:, None] == jnp.arange(positions, dtype=jnp.int32)[None, :]).astype(
        jnp.bfloat16
    )
    placed = jnp.dot(position_pick, pos_table, preferred_element_type=jnp.float32).reshape(
        tiles.shape
    )
    hidden = (tiles.astype(jnp.float32) + placed).astype(jnp.bfloat16)
    start = hidden[0].transpose(1, 2, 0, 3)

    cells = height * breadth
    tokens = frames * cells
    pack = jnp.concatenate(
        [
            w_keyval.reshape(depth, 2, C, -1).transpose(2, 0, 1, 3).reshape(C, depth, -1),
            w_query.reshape(depth, C, -1).transpose(1, 0, 2),
        ],
        axis=2,
    )
    actions = action_table.shape[0]
    assert actions == 8
    aux = jnp.concatenate(
        [action_table, dyn_gain[None], jnp.zeros((7, action_table.shape[1]), jnp.bfloat16)], axis=0
    )
    pick = (
        jnp.tile(action_ids[:, None, :], (1, cells, 1)).reshape(-1)[:, None] == jnp.arange(16, dtype=jnp.int32)[None]
    ).astype(jnp.bfloat16)
    width = pack.shape[2]
    qcols = group * HEAD
    bf16, f32 = jnp.bfloat16, jnp.float32
    dma = pltpu.SemaphoreType.DMA
    out = pl.pallas_call(
        functools.partial(window_kernel, (D, C, T, (2 + group // 2) * HEAD)),
        out_shape=jax.ShapeDtypeStruct((D * tokens, C * qcols), bf16),
        in_specs=[pl.BlockSpec(memory_space=pltpu.VMEM)] * 8,
        out_specs=pl.BlockSpec(memory_space=pltpu.VMEM),
        scratch_shapes=[
            pltpu.VMEM((S * depth, width), bf16),
            pltpu.VMEM((channels, DIM), bf16),
            pltpu.VMEM((16, DIM), bf16),
            pltpu.VMEM((C, D * tokens, channels), bf16),
            pltpu.VMEM((C, D * tokens, DIM), bf16),
            pltpu.VMEM((C, D * tokens, HEAD), f32),
            pltpu.VMEM((C, D * tokens, qcols), bf16),
            pltpu.VMEM((C, D * tokens, HEAD), bf16),
            pltpu.VMEM((C, D * tokens, HEAD), bf16),
            pltpu.VMEM((blocks, 2, breadth, frames, channels), bf16),
            pltpu.VMEM((max(blocks - 1, 1), height, breadth, frames, channels), bf16),
            pltpu.VMEM((tokens, channels), f32),
            pltpu.VMEM((tokens, channels), bf16),
            dma((blocks, 2)),
            dma((blocks, 2)),
            dma((C, T, 4)),
            dma((C, T, 4)),
            dma((C, T, D, 2)),
            dma((C, T, D, 2)),
            dma((C, D)),
            dma((C, D)),
            dma((D,)),
            dma((D,)),
            dma((C, 2)),
            dma((C, 2)),
            dma((4,)),
            dma((C + 1,)),
            dma((C + 1,)),
        ],
        compiler_params=pltpu.CompilerParams(
            collective_id=0, has_side_effects=True, vmem_limit_bytes=60 * 1024 * 1024
        ),
    )(pack, w_in, aux, start, depth_kernel, enc_gain, point_weight, pick)
    out = out.reshape(D, height, breadth, frames, -1).transpose(frames_first)
    return jnp.take(out, seq_order, axis=3)


def solution(mesh):
    placed = (
        P("dp", None, "seq", None, None),
        P("dp", None, "seq", None),
        P(),
        P(),
        P(),
        P(),
        P(),
        P("seq", "dp"),
        P(None, "dp"),
        P("dp"),
        P("seq", "dp"),
        P("seq", None, "dp"),
        P(),
    )
    return jax.shard_map(
        body,
        mesh=mesh,
        in_specs=placed,
        out_specs=P(None, None, "seq", None, "dp"),
        check_vma=False,
    )
```

time: 210 us -> 179 us (0.85)
  Pallas kernels: 194 us -> 162 us
    pallas_call x1, Pallas kernels: 194 us -> 162 us  [body(): pl.pallas_call(functools.partial(window_kernel, (D, C, T, (2 + group // 2...]
where the time goes in v1:
time: 179 us; the launch traced here: 178 us
  Pallas kernels  162 us (91%)
  local copies, waits for them, and re-layouts  10.7 us (6%)
  other arithmetic  4.36 us (2%)
    pallas_call x1, Pallas kernels, body(): pl.pallas_call(functools.partial(window_kernel, (D, C, T, (2 + group // 2...  162 us

profile of v1, /device:TPU:11, one launch (start us, length us, event | category | flops | bytes accessed | tf_op | source)
XLA Modules:
  0.0 177.6 jit_solution(13555988553879231476)
XLA Ops:
  0.0 0.0 copy-start
  0.0 1.6 copy.35
  1.6 0.0 copy-done
  1.7 1.3 bitcast_bitcast_fusion.1
  2.9 2.2 %reshape.28 = bf16[4,320,256]{2,1,0:T(8,128)(2,1)S(1)} reshape(bf16[4,320,2,128]{3,2,1,0:T(2,128)(2,1)} %bitcast_bitcast_fusion.1) | data formatting | bytes 1310720 | tf_op jit(solution)/shard_map/reshape | solution.py:601
  5.2 0.0 copy-start.6
  5.2 0.0 copy-start.1
  5.2 1.6 pad_maximum_fusion.pack_ref
  6.8 0.0 copy-done.6
  6.8 0.0 copy-start.4
  6.8 0.1 copy.21
  6.9 0.1 eq.28
  7.0 0.0 copy-done.1
  7.0 0.0 copy-start.7
  7.0 0.3 fusion.3
  7.3 0.1 reshape.30
  7.5 0.3 copy-done.2
  7.7 1.1 fusion.1.start_ref
  8.9 0.0 copy-done.3
  8.9 0.7 copy.23.taps_ref
  9.5 0.0 copy-done.5
  9.6 0.1 pad.2.clone
  9.6 0.0 copy-done.4
  9.6 0.7 maximum_maximum_fusion.aux_ref
  10.4 0.0 copy-done.7
  10.4 0.1 tile.8
  10.5 0.7 fusion.2.pick_ref
  11.2 162.2 %shard_map.127 = bf16[256,2560]{1,0:T(8,128)(2,1)} custom-call(bf16[4,320,896]{2,1,0:T(8,128)(2,1)} %pad_maximum_fusion.pack_ref, bf16[64,2560]{1,0:T(8,128)(2,1)} %in_ref.1, bf16[16,2560]{1,0:T(8,128)(2,1)} %maximum_maximum_fusion.aux_ref, bf16[2,4,16,1024]{3,2,1,0:T(8,128)(2,1)} %fusion.1.start_ref, bf16[2,27,1024]{2,1,0:T(8,128)(2,1)} %copy.23.taps_ref, ...), custom_call_target="tpu_custom_call" | custom-call | tf_op jit(solution)/shard_map/pallas_call | solution.py:618
  173.3 0.0 copy-done.8
  173.4 1.9 %gather_fusion = bf16[4,2,16,2,2560]{4,2,3,1,0:T(8,128)(2,1)S(1)} fusion(bf16[2,16,2,4,2560]{4,1,3,2,0:T(8,128)(2,1)} %bitcast.25, s32[1024]{0:T(1024)S(1)} %pad_clamp_fusion), kind=kCustom, calls=%fused_computation | custom fusion | bytes 2621456 | tf_op jit(solution)/shard_map/jit(_take)/gather | solution.py:658
  175.3 0.2 select_bitcast_fusion
  175.5 2.1 %copy.24 = bf16[2,16,2,4,2560]{4,3,2,1,0:T(4,128)(2,1)} copy(bf16[2,16,2,4,2560]{4,1,2,0,3:T(8,128)(2,1)S(1)} %select_bitcast_fusion) | data formatting | bytes 2621440 | tf_op jit(solution)/shard_map/jit(_take)/select_n | solution.py:658
  (10 shorter events, 0.1 us)
Async XLA Ops:
  0.0 1.6 copy-start
  5.2 1.6 copy-start.6
  5.2 1.8 %copy-start.1 = (bf16[128,1024]{1,0:T(8,128)(2,1)S(1)}, bf16[128,1024]{1,0:T(8,128)(2,1)}, u32[]{:S(2)}) copy-start(bf16[128,1024]{1,0:T(8,128)(2,1)} %param.15) | copy-start | bytes 786436
  6.8 1.0 copy-start.2
  6.8 2.1 %copy-start.3 = (bf16[2,27,1024]{2,0,1:T(2,128)(2,1)S(1)}, bf16[2,27,1024]{2,0,1:T(2,128)(2,1)}, u32[]{:S(2)}) copy-start(bf16[2,27,1024]{2,0,1:T(2,128)(2,1)} %param.16) | copy-start | bytes 331780
  6.8 2.8 %copy-start.5 = (bf16[2560]{0:T(1024)(128)(2,1)S(1)}, bf16[2560]{0:T(1024)(128)(2,1)}, u32[]{:S(2)}) copy-start(bf16[2560]{0:T(1024)(128)(2,1)} %param.22) | copy-start | bytes 15364
  6.8 2.9 %copy-start.4 = (bf16[8,2560]{1,0:T(8,128)(2,1)S(1)}, bf16[8,2560]{1,0:T(8,128)(2,1)}, u32[]{:S(2)}) copy-start(bf16[8,2560]{1,0:T(8,128)(2,1)} %param.21) | copy-start | bytes 122884
  7.0 3.3 %copy-start.7 = (s32[2,16]{1,0:T(2,128)S(1)}, s32[2,16]{1,0:T(2,128)}, u32[]{:S(2)}) copy-start(s32[2,16]{1,0:T(2,128)} %param.19) | copy-start | bytes 388
  11.2 162.2 %copy-start.8 = (s32[4]{0:T(128)S(1)}, s32[4]{0:T(128)}, u32[]{:S(2)}) copy-start(s32[4]{0:T(128)} %param.25) | copy-start | bytes 52

commit v2 on v1

v2 whole, which is shorter than its diff:
```python
import functools
import math

import jax
import jax.numpy as jnp
from jax import lax
from jax.experimental import pallas as pl
from jax.experimental.pallas import tpu as pltpu
from jax.sharding import PartitionSpec as P

DIM = 5120
HEAD = 128
Q_HEADS = 40
KV_HEADS = 8
MESH = pl.DeviceIdType.MESH


def gelu(z):
    half = 0.5 * z
    return half + half * jnp.tanh(z * (0.7978845608028654 + 0.035677408136300125 * (z * z)))


def flipped(t, mask, bits):
    for bit in bits:
        if mask & bit:
            t = t + bit - 2 * bit * ((t // bit) % 2)
    return t


def window_kernel(
    sizes,
    query_ref,
    keyval_ref,
    in_ref,
    action_ref,
    scale_ref,
    tiles_ref,
    place_ref,
    table_ref,
    taps_ref,
    gains_ref,
    point_hbm,
    ids_ref,
    order_ref,
    out_ref,
    w_all,
    in_all,
    aux_all,
    lat_all,
    embeds,
    squares,
    mixed,
    keys,
    values,
    halos,
    middle,
    conv,
    latent_ref,
    rough,
    start_ref,
    point_ref,
    aux_ref,
    kv_pack,
    place_row,
    ids_row,
    h_send,
    h_recv,
    w_send,
    w_recv,
    i_send,
    i_recv,
    l_send,
    l_recv,
    a_send,
    a_recv,
    o_send,
    o_recv,
    own_sem,
    zi_send,
    zl_send,
):
    D, C, T, edges = sizes
    d = lax.axis_index("dp")
    seq = lax.axis_index("seq")
    c = seq // T
    t = seq % T
    bits = []
    bit = T // 2
    while bit:
        bits.append(bit)
        bit //= 2
    early, last = bits[:-1], bits[-1]
    near_masks = [m for m in range(T) if not m & last]
    near_masks.sort(key=lambda m: m.bit_count())
    depth = query_ref.shape[0]
    in_rows, in_cols = in_ref.shape
    tokens = latent_ref.shape[0]
    rows = D * tokens
    banks = min(C, 2)
    bank = C // banks
    bank_rows = bank * rows
    far = (banks - 1) - c // bank
    near = c // bank
    group = Q_HEADS // KV_HEADS
    qcols = group * HEAD

    orders = [
        sorted(range(C), key=lambda o, i=i: (abs(o - i), o if 2 * i < C else -o)) for i in range(C)
    ]

    def nearest(h):
        value = orders[0][h]
        for i in range(1, C):
            value = jnp.where(c == i, orders[i][h], value)
        return value

    origins = [c] + [nearest(h) for h in range(1, C)]

    def to_c(shift):
        return (d, ((c + shift) % C) * T + t)

    def to_t(bit):
        return (d, c * T + flipped(t, bit, bits))

    def to_d(shift):
        return ((d + shift) % D, seq)

    peers = [to_c(s) for s in range(1, C)] + [to_t(b) for b in bits] + [to_d(s) for s in range(1, D)]
    S = C * T
    above, below = (d, (seq + S - 1) % S), (d, (seq + 1) % S)
    peers += [above, below]
    own = [
        pltpu.make_async_copy(point_hbm, point_ref, own_sem.at[4]),
        pltpu.make_async_copy(
            in_ref,
            in_all.at[
                pl.ds(pl.multiple_of(seq * in_rows, in_rows), in_rows),
                pl.ds(pl.multiple_of(d * in_cols, HEAD), in_cols),
            ],
            own_sem.at[1],
        ),
        pltpu.make_async_copy(
            query_ref.at[:, pl.ds(pl.multiple_of(c * qcols, HEAD), qcols)],
            w_all.at[pl.ds(pl.multiple_of(seq * depth, depth), depth), pl.ds(2 * HEAD, qcols)],
            own_sem.at[0],
        ),
    ]
    point_copy = own.pop(0)
    point_copy.start()
    for copy in own:
        copy.start()
    height, breadth, frames, channels = start_ref.shape
    with jax.named_scope("place"):
        positions = table_ref.shape[0]
        for r in range(height):
            for w in range(breadth):
                base = (r * breadth + w) * frames
                place_row[:, base : base + frames] = place_ref[0, r, w : w + 1, :]
        for k in range(D):
            ids_row[:, k * frames : (k + 1) * frames] = ids_ref[k : k + 1, :]
        chosen = place_row[...] == lax.broadcasted_iota(jnp.int32, (positions, tokens), 0)
        placed = lax.dot_general(
            jnp.where(chosen, 1.0, 0.0).astype(jnp.bfloat16),
            table_ref[...],
            (((0,), (0,)), ((), ())),
            preferred_element_type=jnp.float32,
        )
        for r in range(height):
            for w in range(breadth):
                base = (r * breadth + w) * frames
                tile = tiles_ref[0, :, r, w, :].astype(jnp.float32)
                start_ref[r, w] = (tile + placed[base : base + frames]).astype(jnp.bfloat16)
        actions = action_ref.shape[0]
        aux_ref[:actions] = action_ref[...]
        for k in range(in_cols // HEAD):
            aux_ref[actions:, k * HEAD : (k + 1) * HEAD] = jnp.broadcast_to(
                scale_ref[k : k + 1, :], (16 - actions, HEAD)
            )

    with jax.named_scope("barrier"):
        barrier = pltpu.get_barrier_semaphore()
        for peer in peers:
            pl.semaphore_signal(barrier, inc=1, device_id=peer, device_id_type=MESH)
        pl.semaphore_wait(barrier, len(peers))

    log = []
    waiting = []

    def run(guard, event, *args):
        if not waiting:
            log.append((guard, event, args))
        if guard is None:
            event(*args)
        else:
            pl.when(guard)(functools.partial(event, *args))

    def push(src, dst, send_sem, recv_sem, peer):
        copy = pltpu.make_async_remote_copy(
            src_ref=src,
            dst_ref=dst,
            send_sem=send_sem,
            recv_sem=recv_sem,
            device_id=peer,
            device_id_type=MESH,
        )
        if waiting:
            copy.wait_send()
        else:
            copy.start()

    def arrived(ref, sem):
        if not waiting:
            pltpu.make_async_copy(ref, ref, sem).wait()

    w_cols = [(first, last_col - first) for first, last_col in zip(edges, edges[1:])]
    stages = len(w_cols)
    pieces = [(0, 0, 2 * HEAD)]
    pieces += [(g, max(first, 2 * HEAD), min(count, first + count - 2 * HEAD)) for g, (first, count) in enumerate(w_cols)]

    def w_slot(o, m, piece):
        g, first, count = piece
        origin = o * T + flipped(t, m, bits)
        return w_all.at[
            pl.ds(pl.multiple_of(origin * depth, depth), depth), pl.ds(first, count)
        ]

    def w_own(target, piece):
        g, first, count = piece
        if first == 0:
            return kv_pack.at[target]
        column = target * qcols + first - 2 * HEAD
        return query_ref.at[:, pl.ds(pl.multiple_of(column, HEAD), count)]

    split = in_rows // 2
    WHOLE, HEAD_PART, TAIL_PART = 0, 1, 2

    def part_rows(part):
        return ((0, in_rows), (0, split), (split, in_rows - split))[part]

    def i_slot(o, m, e, part):
        first, count = part_rows(part)
        origin = o * T + flipped(t, m, bits)
        column = ((d + D - e) % D) * in_cols
        return in_all.at[
            pl.ds(pl.multiple_of(origin * in_rows + first, math.gcd(in_rows, split)), count),
            pl.ds(pl.multiple_of(column, HEAD), in_cols),
        ]

    def l_slot(o, e):
        row = ((d + D - e) % D) * tokens
        return lat_all.at[pl.ds(pl.multiple_of(o * rows + row, tokens), tokens)]

    def a_slot(e):
        column = ((d + D - e) % D) * in_cols
        return aux_all.at[:, pl.ds(pl.multiple_of(column, HEAD), in_cols)]

    hops = [(k, way) for k in range(1, C) for way in (1, -1)]

    def hop_origin(k, way):
        return c - way * k

    def hop_guard(k, way):
        return c >= k if way > 0 else c + k < C

    def onward(way):
        return (d, (c + way) * T + t), (c + 1 < C if way > 0 else c >= 1)

    def z_own(src, dst, send_sems, recv_sem):
        for k, way in enumerate((1, -1)):
            if C > 1:
                peer, guard = onward(way)
                pl.when(guard)(functools.partial(push, src, dst, send_sems.at[k], recv_sem, peer))

    def z_hop(slot, send_sem, recv_sem, way):
        peer, guard = onward(way)
        pl.when(guard)(functools.partial(push, slot, slot, send_sem, recv_sem, peer))

    def w_forward(o, m, piece, src):
        k = pieces.index(piece)
        low = -1
        for b in bits:
            if m & b:
                low = bits.index(b)
        for b in bits[low + 1 :]:
            push(src, w_slot(o, m, piece), w_send.at[o, m | b, k], w_recv.at[o, m | b, k], to_t(b))

    def w_across(h, piece):
        k = pieces.index(piece)
        target = origins[h]
        push(
            w_own(target, piece),
            w_slot(c, 0, piece),
            w_send.at[target, 0, k],
            w_recv.at[c, 0, k],
            (d, target * T + t),
        )

    def i_push(o, m, e, part, own, new_m, new_e, peer):
        first, count = part_rows(part)
        src = in_ref.at[pl.ds(first, count)] if own else i_slot(o, m, e, part)
        k = int(part == TAIL_PART)
        push(src, i_slot(o, m, e, part), i_send.at[o, new_m, new_e, k], i_recv.at[o, new_m, new_e, k], peer)

    def i_forward(o, m, e, part, own=False):
        if m & last:
            return
        low = -1
        for b in early:
            if m & b:
                low = early.index(b)
        later = early[low + 1 :]
        if e == 0:
            for b in later:
                i_push(o, m, e, WHOLE, own, m | b, e, to_t(b))
            for shift in range(1, D):
                i_push(o, m, e, HEAD_PART if m else WHOLE, own, m, shift, to_d(shift))
        elif m == 0 or part == TAIL_PART:
            for b in later:
                i_push(o, m, e, TAIL_PART, own, m | b, e, to_t(b))
        i_push(o, m, e, part, own, m | last, e, to_t(last))

    def l_forward(o, src):
        for e in range(1, D):
            push(src, l_slot(o, 0), l_send.at[o, e], l_recv.at[o, e], to_d(e))

    def share_rows(l, source):
        push(source.at[height - 1], halos.at[l, 0], h_send.at[l, 0], h_recv.at[l, 0], below)
        push(source.at[0], halos.at[l, 1], h_send.at[l, 1], h_recv.at[l, 1], above)

    def start_own():
        z_own(in_ref, i_slot(c, 0, 0, WHOLE), zi_send, i_recv.at[c, 0, 0, 0])
        i_forward(c, 0, 0, WHOLE, True)
        for shift in range(1, D):
            push(aux_ref, a_slot(0), a_send.at[shift], a_recv.at[shift], to_d(shift))

    own.append(pltpu.make_async_copy(aux_ref, a_slot(0), own_sem.at[3]))
    own[-1].start()
    run(None, share_rows, 0, start_ref)
    run(None, start_own)

    def i_event(o, m, e, part=0):
        arrived(i_slot(o, m, e, part), i_recv.at[o, m, e, int(part == TAIL_PART)])
        i_forward(o, m, e, part)

    def iz_event(k, way):
        o = hop_origin(k, way)
        slot = i_slot(o, 0, 0, WHOLE)
        arrived(slot, i_recv.at[o, 0, 0, 0])
        z_hop(slot, zi_send.at[2 * k + (way > 0)], i_recv.at[o, 0, 0, 0], way)
        i_forward(o, 0, 0, WHOLE)

    def lz_event(k, way):
        o = hop_origin(k, way)
        slot = l_slot(o, 0)
        arrived(slot, l_recv.at[o, 0])
        z_hop(slot, zl_send.at[2 * k + (way > 0)], l_recv.at[o, 0], way)
        l_forward(o, slot)

    def local_event(k, way):
        o = hop_origin(k, way)
        for m in near_masks:
            if m:
                i_event(o, m, 0)
        for e in range(1, D):
            i_event(o, 0, e)

    def both_ways(event, k):
        with jax.named_scope("%s%d" % (event.__name__[:2], k)):
            for way in (1, -1) if 0 < k < C else ():
                run(hop_guard(k, way), event, k, way)

    def w_event(h, m, piece):
        o = origins[h]
        slot = w_slot(o, m, piece)
        arrived(slot, w_recv.at[o, m, pieces.index(piece)])
        w_forward(o, m, piece, slot)

    def w_forward_own(piece):
        w_forward(c, 0, piece, w_own(c, piece))

    w_pushes = []
    for piece in pieces:
        w_pushes += [(h, piece) for h in range(C - 1, -1, -1)]

    def w_start(count):
        for h, piece in w_pushes[:count]:
            if h:
                run(None, w_across, h, piece)
            else:
                run(None, w_forward_own, piece)
        del w_pushes[:count]

    lanes = 256

    def encode(l, source):
        arrived(halos.at[l, 0], h_recv.at[l, 0])
        arrived(halos.at[l, 1], h_recv.at[l, 1])
        frame_ids = lax.broadcasted_iota(jnp.int32, (frames, lanes), 0)

        def lane_step(j, carry):
            cols = pl.ds(pl.multiple_of(j * lanes, lanes), lanes)
            taps = [taps_ref[k, l : l + 1, cols].astype(jnp.float32) for k in range(27)]

            def patch(r, w):
                if r < 0:
                    return jnp.where(seq > 0, halos[l, 0, w, :, cols].astype(jnp.float32), 0.0)
                if r == height:
                    return jnp.where(seq < S - 1, halos[l, 1, w, :, cols].astype(jnp.float32), 0.0)
                return source[r, w, :, cols].astype(jnp.float32)

            for r in range(height):
                for w in range(breadth):
                    sums = [None] * 3
                    for b in range(3):
                        for k in range(3):
                            if not 0 <= w + k - 1 < breadth:
                                continue
                            value = patch(r + b - 1, w + k - 1)
                            for a in range(3):
                                tap = 9 * a + 3 * b + k
                                term = value * taps[tap]
                                sums[a] = term if sums[a] is None else sums[a] + term
                    total = sums[2]
                    for a in range(2):
                        moved = pltpu.roll(sums[a], 2 - a, 0)
                        total = total + jnp.where(frame_ids >= 2 - a, moved, 0.0)
                    base = (r * breadth + w) * frames
                    conv[base : base + frames, cols] = total
            return carry

        lax.fori_loop(0, channels // lanes, lane_step, 0)
        summed = conv[...]
        factor = lax.rsqrt(jnp.mean(summed * summed, axis=-1, keepdims=True) + 1e-05)
        gain = gains_ref[l].astype(jnp.float32)
        normed = (summed * factor * gain[None]).astype(jnp.bfloat16)
        projected = jnp.dot(normed, point_ref[l], preferred_element_type=jnp.float32)
        change = gelu(projected)
        for r in range(height):
            for w in range(breadth):
                base = (r * breadth + w) * frames
                value = source[r, w].astype(jnp.float32) + change[base : base + frames]
                value = value.astype(jnp.bfloat16)
                if l + 1 < point_ref.shape[0]:
                    middle[l, r, w] = value
                else:
                    rough[base : base + frames] = value

    def local_events(h):
        o = origins[h]
        for m in near_masks:
            if m:
                i_event(o, m, 0)
        for e in range(1, D):
            i_event(o, 0, e)

    point_copy.wait()
    source = start_ref
    for l in range(point_ref.shape[0]):
        with jax.named_scope("encode"):
            encode(l, source)
        if l + 1 < point_ref.shape[0]:
            source = middle.at[l]
            run(None, share_rows, l + 1, source)
        if l == 0:
            both_ways(iz_event, 1)
            run(None, local_event, 0, 1)

    with jax.named_scope("order"):
        row_ids = lax.broadcasted_iota(jnp.int32, (tokens, tokens), 0)
        col_ids = lax.broadcasted_iota(jnp.int32, (tokens, tokens), 1)
        row_cells, col_cells = row_ids // frames, col_ids // frames
        wanted = row_cells // breadth * breadth
        for w in range(breadth):
            wanted = wanted + jnp.where(row_cells % breadth == w, order_ref[w], 0)
        moved = (wanted == col_cells) & (row_ids % frames == col_ids % frames)
        latent_ref[...] = jnp.dot(
            jnp.where(moved, 1.0, 0.0).astype(jnp.bfloat16), rough[...], preferred_element_type=jnp.float32
        ).astype(jnp.bfloat16)

    def start_latent():
        z_own(latent_ref, l_slot(c, 0), zl_send, l_recv.at[c, 0])
        l_forward(c, latent_ref)

    run(None, start_latent)
    latent_copy = pltpu.make_async_copy(latent_ref, l_slot(c, 0), own_sem.at[2])
    latent_copy.start()
    own.append(latent_copy)

    def w_events(piece, count):
        with jax.named_scope("w%d_%d" % (pieces.index(piece), count)):
            for m in range(T):
                if (m & ~last).bit_count() + (T if m & last else 0) == count:
                    for h in range(C - 1, -1, -1):
                        if h or m:
                            run(None, w_event, h, m, piece)

    both_ways(iz_event, 2)
    with jax.named_scope("kv"):
        for o in range(C):
            for k in range(2):
                kv_pack[o, :, k * HEAD : (k + 1) * HEAD] = keyval_ref[:, k, o * HEAD : (o + 1) * HEAD]
        own.append(pltpu.make_async_copy(kv_pack.at[c], w_slot(c, 0, pieces[0]), own_sem.at[5]))
        own[-1].start()
    both_ways(local_event, 1)
    both_ways(lz_event, 1)
    both_ways(iz_event, 3)
    both_ways(lz_event, 2)
    w_start(2)
    both_ways(local_event, 2)
    w_start(2)
    both_ways(lz_event, 3)
    w_start(4)
    both_ways(local_event, 3)
    for k in range(4, C):
        for event in (iz_event, local_event, lz_event):
            both_ways(event, k)
    w_start(len(w_pushes))
    steps = len(early) + 1
    w_todo = [(k + 2.5 * count, k, count) for k in range(len(pieces)) for count in range(steps)]
    w_todo = [(pieces[k], count) for _, k, count in sorted(w_todo)]

    def core_events(e):
        with jax.named_scope("core"):
            for h in range(C):
                for m in near_masks:
                    if m and e:
                        run(None, i_event, origins[h], m | last, e, HEAD_PART)
                        run(None, i_event, origins[h], m | last, e, TAIL_PART)
                    else:
                        run(None, i_event, origins[h], m | last, e)

    def cross_events(e):
        with jax.named_scope("cross"):
            for h in range(C):
                for m in near_masks:
                    if m:
                        run(None, i_event, origins[h], m, e, HEAD_PART)
                        run(None, i_event, origins[h], m, e, TAIL_PART)

    chunk = in_cols // 2 if in_cols % (2 * HEAD) == 0 else in_cols
    chosen = ids_row[...] == lax.broadcasted_iota(jnp.int32, (16, D * frames), 0)
    picked = jnp.where(chosen, 1.0, 0.0).astype(jnp.bfloat16)

    def rows_of(which):
        return pl.ds(pl.multiple_of(which * bank_rows, bank_rows), bank_rows)

    def embed_bank(which, e):
        at = rows_of(which)
        first = ((d + D - e) % D) * in_cols
        if e == 0:
            squares[at] = jnp.zeros((bank_rows, HEAD), jnp.float32)

        def step(j, carry):
            cols = pl.ds(pl.multiple_of(first + j * chunk, HEAD), chunk)
            z = jnp.dot(lat_all[at], in_all[:, cols], preferred_element_type=jnp.float32)
            action = lax.dot_general(
                picked,
                aux_all[:, cols],
                (((0,), (0,)), ((), ())),
                preferred_element_type=jnp.float32,
            )
            action = jnp.broadcast_to(
                action.reshape(1, D, 1, frames, chunk),
                (bank, D, tokens // frames, frames, chunk),
            )
            g = gelu(z + action.reshape(bank_rows, chunk))
            gain = aux_all[:, cols].astype(jnp.float32)[8:9]
            embeds[at, cols] = (g * gain).astype(jnp.bfloat16)
            square = g * g
            part = square[:, :HEAD]
            for k in range(1, chunk // HEAD):
                part = part + square[:, k * HEAD : (k + 1) * HEAD]
            squares[at] += part
            return carry

        with jax.named_scope("embed"):
            lax.fori_loop(0, in_cols // chunk, step, 0)

    def take_w(count):
        for item in w_todo[:count]:
            w_events(*item)
        del w_todo[:count]

    core_events(0)
    take_w(1)
    for copy in own:
        copy.wait()
    with jax.named_scope("lx"):
        for h in range(C):
            for k in range(1, D):
                arrived(l_slot(origins[h], k), l_recv.at[origins[h], k])
    embed_bank(far, 0)
    take_w(1)
    if banks > 1:
        embed_bank(near, 0)
    for e in range(1, D):
        cross_events(e)
        take_w(2)
        with jax.named_scope("aux"):
            arrived(a_slot(e), a_recv.at[e])
        core_events(e)
        embed_bank(far, e)
        take_w(2)
        if banks > 1:
            embed_bank(near, e)

    def need_w(g):
        with jax.named_scope("need"):
            while any(piece[0] <= g for piece, count in w_todo):
                take_w(1)
            for piece in pieces:
                if piece[0] == g:
                    for count in range(T, T + steps):
                        w_events(piece, count)

    seen = (row_ids // frames == col_ids // frames) & (row_ids >= col_ids)

    pair = jnp.where(
        lax.broadcasted_iota(jnp.int32, (2 * HEAD, 2 * HEAD), 0) // HEAD
        == lax.broadcasted_iota(jnp.int32, (2 * HEAD, 2 * HEAD), 1) // HEAD,
        1.0,
        0.0,
    ).astype(jnp.bfloat16)

    def unit(x):
        width = x.shape[1]
        total = jnp.dot(
            (x * x).astype(jnp.bfloat16), pair[:width, :width], preferred_element_type=jnp.float32
        )
        return x * lax.rsqrt(total * (1.0 / HEAD) + 1e-06)

    def mix_bank(which, g):
        first, count = w_cols[g]
        base = which * bank_rows
        at = rows_of(which)
        total = jnp.dot(
            embeds[at], w_all[:, first : first + count], preferred_element_type=jnp.float32
        )
        mean = jnp.sum(squares[at], axis=-1, keepdims=True) / DIM
        total = total * lax.rsqrt(mean + 1e-05)
        if g == 0:
            keys[at] = unit(total[:, :HEAD]).astype(jnp.bfloat16)
            values[at, :HEAD] = total[:, HEAD : 2 * HEAD].astype(jnp.bfloat16)
            values[at, HEAD:] = jnp.ones((bank_rows, HEAD), jnp.bfloat16)
        key, value = keys[at], values[at]
        left = 2 * HEAD if g == 0 else 0
        while left < count:
            width = min(2 * HEAD, count - left)
            query = (unit(total[:, left : left + width]) * HEAD**-0.5).astype(jnp.bfloat16)
            for inner in range(0, width, HEAD):
                to = first + left + inner - 2 * HEAD
                spans = [slice(i, i + tokens) for i in range(0, bank_rows, tokens)]
                scores = [
                    lax.dot_general(
                        query[span, inner : inner + HEAD],
                        key[span],
                        (((1,), (1,)), ((), ())),
                        preferred_element_type=jnp.float32,
                    )
                    for span in spans
                ]
                raised = [
                    jnp.where(seen, jnp.exp(score), 0.0).astype(jnp.bfloat16) for score in scores
                ]
                for i, span in enumerate(spans):
                    both = jnp.dot(raised[i], value[span], preferred_element_type=jnp.float32)
                    result = (both[:, :HEAD] / both[:, HEAD:]).astype(jnp.bfloat16)
                    mixed[pl.ds(pl.multiple_of(base + i * tokens, tokens), tokens), to : to + HEAD] = result
            left += width

    def out_cols(g):
        first, count = w_cols[g]
        return (0, count - 2 * HEAD) if g == 0 else (first - 2 * HEAD, count)

    def block_rows(where):
        return pl.ds(pl.multiple_of(where * rows, rows), rows)

    def send_of(where, g):
        first, count = out_cols(g)
        return pltpu.make_async_remote_copy(
            src_ref=mixed.at[block_rows(where), pl.ds(first, count)],
            dst_ref=out_ref.at[:, pl.ds(pl.multiple_of(c * qcols + first, HEAD), count)],
            send_sem=o_send.at[where, g],
            recv_sem=o_recv.at[c, g],
            device_id=(d, where * T + t),
            device_id_type=MESH,
        )

    far_blocks = [far * bank + j for j in range(bank)] if banks > 1 else []
    near_blocks = [near * bank + (c + j) % bank for j in range(1, bank)]

    for g in range(stages):
        need_w(g)
        for which, blocks in ((far, far_blocks), (near, near_blocks))[2 - banks :]:
            with jax.named_scope("mix"):
                mix_bank(which, g)
            for where in blocks:
                send_of(where, g).start()
    keep = pltpu.make_async_copy(
        mixed.at[block_rows(c)],
        out_ref.at[:, pl.ds(pl.multiple_of(c * qcols, HEAD), qcols)],
        own_sem.at[0],
    )
    keep.start()
    with jax.named_scope("tail"):
        for g in range(stages):
            first, count = out_cols(g)
            for where in near_blocks + far_blocks:
                send_of(where, g).wait_send()
                column = where * qcols + first
                arrived(
                    out_ref.at[:, pl.ds(pl.multiple_of(column, HEAD), count)], o_recv.at[where, g]
                )
        keep.wait()
    waiting.append(True)
    for guard, event, args in log:
        run(guard, event, *args)


def body(
    tiles,
    patch_index,
    pos_table,
    depth_kernel,
    enc_gain,
    point_weight,
    action_ids,
    w_in,
    action_table,
    dyn_gain,
    w_query,
    w_keyval,
    seq_order,
):
    clip_local, frames, height, breadth, channels = tiles.shape
    positions = pos_table.shape[0]
    blocks = depth_kernel.shape[0]
    D, S = lax.axis_size("dp"), lax.axis_size("seq")
    kv_local = w_keyval.shape[2] // HEAD
    C = math.gcd(kv_local, S)
    T = S // C
    assert T & (T - 1) == 0 and T > 1 and clip_local == 1 and kv_local == C
    group = Q_HEADS // KV_HEADS
    depth = w_query.shape[0]

    cells = height * breadth
    tokens = frames * cells
    assert action_table.shape[0] == 8 and depth_kernel.shape[1] == 27
    width = (2 + group) * HEAD
    qcols = group * HEAD
    bf16, f32 = jnp.bfloat16, jnp.float32
    dma = pltpu.SemaphoreType.DMA
    out = pl.pallas_call(
        functools.partial(window_kernel, (D, C, T, [x * HEAD for x in (0, 2 + group // 2, 1 + group, 2 + group)])),
        out_shape=jax.ShapeDtypeStruct((D * tokens, C * qcols), bf16),
        in_specs=[
            pl.BlockSpec(memory_space=space)
            for space in [pl.ANY, pltpu.VMEM, pl.ANY]
            + [pltpu.VMEM] * 7
            + [pl.ANY, pltpu.VMEM, pltpu.SMEM]
        ],
        out_specs=pl.BlockSpec(memory_space=pltpu.VMEM),
        scratch_shapes=[
            pltpu.VMEM((S * depth, width), bf16),
            pltpu.VMEM((channels, DIM), bf16),
            pltpu.VMEM((16, DIM), bf16),
            pltpu.VMEM((C * D * tokens, channels), bf16),
            pltpu.VMEM((C * D * tokens, DIM), bf16),
            pltpu.VMEM((C * D * tokens, HEAD), f32),
            pltpu.VMEM((C * D * tokens, qcols), bf16),
            pltpu.VMEM((C * D * tokens, HEAD), bf16),
            pltpu.VMEM((C * D * tokens, 2 * HEAD), bf16),
            pltpu.VMEM((blocks, 2, breadth, frames, channels), bf16),
            pltpu.VMEM((max(blocks - 1, 1), height, breadth, frames, channels), bf16),
            pltpu.VMEM((tokens, channels), f32),
            pltpu.VMEM((tokens, channels), bf16),
            pltpu.VMEM((tokens, channels), bf16),
            pltpu.VMEM((height, breadth, frames, channels), bf16),
            pltpu.VMEM(point_weight.shape, bf16),
            pltpu.VMEM((16, w_in.shape[1]), bf16),
            pltpu.VMEM((C, depth, 2 * HEAD), bf16),
            pltpu.VMEM((1, tokens), jnp.int32),
            pltpu.VMEM((1, D * frames), jnp.int32),
            dma((blocks, 2)),
            dma((blocks, 2)),
            dma((C, T, 4)),
            dma((C, T, 4)),
            dma((C, T, D, 2)),
            dma((C, T, D, 2)),
            dma((C, D)),
            dma((C, D)),
            dma((D,)),
            dma((D,)),
            dma((C, 3)),
            dma((C, 3)),
            dma((6,)),
            dma((2 * C,)),
            dma((2 * C,)),
        ],
        compiler_params=pltpu.CompilerParams(
            collective_id=0, has_side_effects=True, vmem_limit_bytes=60 * 1024 * 1024
        ),
    )(
        w_query,
        w_keyval,
        w_in,
        action_table,
        dyn_gain.reshape(-1, HEAD),
        tiles,
        patch_index.transpose(0, 2, 3, 1),
        pos_table,
        depth_kernel.transpose(1, 0, 2),
        enc_gain,
        point_weight,
        action_ids,
        seq_order,
    )
    return out.reshape(D, height, breadth, frames, -1).transpose(0, 3, 1, 2, 4)


def solution(mesh):
    placed = (
        P("dp", None, "seq", None, None),
        P("dp", None, "seq", None),
        P(),
        P(),
        P(),
        P(),
        P(),
        P("seq", "dp"),
        P(None, "dp"),
        P("dp"),
        P("seq", "dp"),
        P("seq", None, "dp"),
        P(),
    )
    return jax.shard_map(
        body,
        mesh=mesh,
        in_specs=placed,
        out_specs=P(None, None, "seq", None, "dp"),
        check_vma=False,
    )
```

time: 179 us -> 139 us (0.78)
  Pallas kernels: 162 us -> 135 us
  local copies, waits for them, and re-layouts: 10.7 us -> 3.39 us
  other arithmetic: 4.36 us -> 0 us
    pallas_call x1, Pallas kernels: 162 us -> 135 us  [body(): pl.pallas_call(functools.partial(window_kernel, (D, C, T, [x * HEAD for x...]
    concatenate x2 -> x0, other arithmetic: 2.3 us -> none  [the longest x1 1.59 us: body(): jnp.concatenate([w_keyval.reshape(depth, 2, C, -1).transpose(2, 0, 1, 3)....]
    select_n x1 -> x0, local copies, waits for them, and re-layouts: 2.07 us -> none  [body(): return jnp.take(out, seq_order, axis=3)]
    gather x1 -> x0, local copies, waits for them, and re-layouts: 1.95 us -> none  [body(): return jnp.take(out, seq_order, axis=3)]
    reshape x3 -> x1, local copies, waits for them, and re-layouts: 4 us -> 3.39 us  [body(): return out.reshape(D, height, breadth, frames, -1).transpose(0, 3, 1, 2, 4)]
where the time goes in v2:
time: 139 us
  Pallas kernels  135 us (97%)
  local copies, waits for them, and re-layouts  3.39 us (2%)
    pallas_call x1, Pallas kernels, body(): pl.pallas_call(functools.partial(window_kernel, (D, C, T, [x * HEAD for x...  135 us
    reshape x1, local copies, waits for them, and re-layouts, body(): return out.reshape(D, height, breadth, frames, -1).transpose(0, 3, 1, 2, 4)  3.39 us

profile of v2, /device:TPU:11, one launch (start us, length us, event | category | flops | bytes accessed | tf_op | source)
XLA Modules:
  0.0 138.5 jit_solution(12370738386689905914)
XLA Ops:
  0.0 135.1 %shard_map.127 = bf16[256,2560]{1,0:T(8,128)(2,1)} custom-call(bf16[320,2560]{1,0:T(8,128)(2,1)} %query_ref.1, bf16[320,2,512]{2,1,0:T(2,128)(2,1)} %keyval_ref.1, bf16[64,2560]{1,0:T(8,128)(2,1)} %in_ref.1, bf16[8,2560]{1,0:T(8,128)(2,1)} %action_ref.1, bf16[20,128]{1,0:T(8,128)(2,1)} %bitcast.9, bf16[1,16,2,4,1024]{4,3,2,1,0:T(4,128)(2,1)} %tiles_ref.1, ...), custom_call_target="tpu_custom_call" | custom-call | tf_op jit(solution)/shard_map/pallas_call | solution.py:753
  135.1 3.4 %copy.16 = bf16[2,2,4,16,2560]{4,2,1,3,0:T(4,128)(2,1)} copy(bf16[2,2,4,16,2560]{4,3,2,1,0:T(8,128)(2,1)} %bitcast.7) | data formatting | bytes 2621440 | tf_op jit(solution)/shard_map/reshape | solution.py:818

commit v3 on v2

--- a/solution.py
+++ b/solution.py
@@ -445,14 +445,6 @@
                 else:
                     rough[base : base + frames] = value
 
-    def local_events(h):
-        o = origins[h]
-        for m in near_masks:
-            if m:
-                i_event(o, m, 0)
-        for e in range(1, D):
-            i_event(o, 0, e)
-
     point_copy.wait()
     source = start_ref
     for l in range(point_ref.shape[0]):
@@ -462,17 +454,27 @@
             source = middle.at[l]
             run(None, share_rows, l + 1, source)
         if l == 0:
+            with jax.named_scope("kv"):
+                for o in range(C):
+                    for k in range(2):
+                        kv_pack[o, :, k * HEAD : (k + 1) * HEAD] = keyval_ref[
+                            :, k, o * HEAD : (o + 1) * HEAD
+                        ]
+            own.append(
+                pltpu.make_async_copy(kv_pack.at[c], w_slot(c, 0, pieces[0]), own_sem.at[5])
+            )
+            own[-1].start()
             both_ways(iz_event, 1)
-            run(None, local_event, 0, 1)
 
     with jax.named_scope("order"):
         row_ids = lax.broadcasted_iota(jnp.int32, (tokens, tokens), 0)
         col_ids = lax.broadcasted_iota(jnp.int32, (tokens, tokens), 1)
-        row_cells, col_cells = row_ids // frames, col_ids // frames
+        cells = tokens // frames
+        row_cells = row_ids % cells
         wanted = row_cells // breadth * breadth
         for w in range(breadth):
             wanted = wanted + jnp.where(row_cells % breadth == w, order_ref[w], 0)
-        moved = (wanted == col_cells) & (row_ids % frames == col_ids % frames)
+        moved = (wanted == col_ids // frames) & (row_ids // cells == col_ids % frames)
         latent_ref[...] = jnp.dot(
             jnp.where(moved, 1.0, 0.0).astype(jnp.bfloat16), rough[...], preferred_element_type=jnp.float32
         ).astype(jnp.bfloat16)
@@ -482,6 +484,7 @@
         l_forward(c, latent_ref)
 
     run(None, start_latent)
+    run(None, local_event, 0, 1)
     latent_copy = pltpu.make_async_copy(latent_ref, l_slot(c, 0), own_sem.at[2])
     latent_copy.start()
     own.append(latent_copy)
@@ -495,12 +498,6 @@
                             run(None, w_event, h, m, piece)
 
     both_ways(iz_event, 2)
-    with jax.named_scope("kv"):
-        for o in range(C):
-            for k in range(2):
-                kv_pack[o, :, k * HEAD : (k + 1) * HEAD] = keyval_ref[:, k, o * HEAD : (o + 1) * HEAD]
-        own.append(pltpu.make_async_copy(kv_pack.at[c], w_slot(c, 0, pieces[0]), own_sem.at[5]))
-        own[-1].start()
     both_ways(local_event, 1)
     both_ways(lz_event, 1)
     both_ways(iz_event, 3)
@@ -560,8 +557,8 @@
                 preferred_element_type=jnp.float32,
             )
             action = jnp.broadcast_to(
-                action.reshape(1, D, 1, frames, chunk),
-                (bank, D, tokens // frames, frames, chunk),
+                action.reshape(1, D, frames, 1, chunk),
+                (bank, D, frames, cells, chunk),
             )
             g = gelu(z + action.reshape(bank_rows, chunk))
             gain = aux_all[:, cols].astype(jnp.float32)[8:9]
@@ -582,27 +579,29 @@
         del w_todo[:count]
 
     core_events(0)
-    take_w(1)
     for copy in own:
         copy.wait()
-    with jax.named_scope("lx"):
-        for h in range(C):
-            for k in range(1, D):
-                arrived(l_slot(origins[h], k), l_recv.at[origins[h], k])
+
+    def lat_bank(inside):
+        with jax.named_scope("lx"):
+            for h in range(bank) if inside else range(bank, C):
+                for k in range(1, D):
+                    arrived(l_slot(origins[h], k), l_recv.at[origins[h], k])
+
+    if banks > 1:
+        lat_bank(True)
+        embed_bank(near, 0)
+    take_w(1)
+    lat_bank(False) if banks > 1 else lat_bank(True)
     embed_bank(far, 0)
     take_w(1)
-    if banks > 1:
-        embed_bank(near, 0)
     for e in range(1, D):
         cross_events(e)
-        take_w(2)
         with jax.named_scope("aux"):
             arrived(a_slot(e), a_recv.at[e])
         core_events(e)
         embed_bank(far, e)
-        take_w(2)
-        if banks > 1:
-            embed_bank(near, e)
+    take_w(3)
 
     def need_w(g):
         with jax.named_scope("need"):
@@ -613,7 +612,7 @@
                     for count in range(T, T + steps):
                         w_events(piece, count)
 
-    seen = (row_ids // frames == col_ids // frames) & (row_ids >= col_ids)
+    seen = (row_ids % cells == col_ids % cells) & (row_ids >= col_ids)
 
     pair = jnp.where(
         lax.broadcasted_iota(jnp.int32, (2 * HEAD, 2 * HEAD), 0) // HEAD
@@ -696,6 +695,9 @@
                 mix_bank(which, g)
             for where in blocks:
                 send_of(where, g).start()
+            if g == 0 and blocks is far_blocks:
+                for e in range(1, D):
+                    embed_bank(near, e)
     keep = pltpu.make_async_copy(
         mixed.at[block_rows(c)],
         out_ref.at[:, pl.ds(pl.multiple_of(c * qcols, HEAD), qcols)],
@@ -815,7 +817,7 @@
         action_ids,
         seq_order,
     )
-    return out.reshape(D, height, breadth, frames, -1).transpose(0, 3, 1, 2, 4)
+    return out.reshape(D, frames, height, breadth, -1)
 
 
 def solution(mesh):

time: 139 us -> 138 us (level)
  no operation moved by 1% of the time
where the time goes in v3:
time: 138 us
  Pallas kernels  135 us (98%)
  local copies, waits for them, and re-layouts  3.5 us (3%)
    pallas_call x1, Pallas kernels, body(): pl.pallas_call(functools.partial(window_kernel, (D, C, T, [x * HEAD for x...  135 us
    reshape x1, local copies, waits for them, and re-layouts, body(): return out.reshape(D, frames, height, breadth, -1)  3.5 us

profile of v3, /device:TPU:11, one launch (start us, length us, event | category | flops | bytes accessed | tf_op | source)
XLA Modules:
  0.0 138.1 jit_solution(3112275821114199534)
XLA Ops:
  0.0 134.6 %shard_map.127 = bf16[256,2560]{1,0:T(8,128)(2,1)} custom-call(bf16[320,2560]{1,0:T(8,128)(2,1)} %query_ref.1, bf16[320,2,512]{2,1,0:T(2,128)(2,1)} %keyval_ref.1, bf16[64,2560]{1,0:T(8,128)(2,1)} %in_ref.1, bf16[8,2560]{1,0:T(8,128)(2,1)} %action_ref.1, bf16[20,128]{1,0:T(8,128)(2,1)} %bitcast.4, bf16[1,16,2,4,1024]{4,3,2,1,0:T(4,128)(2,1)} %tiles_ref.1, ...), custom_call_target="tpu_custom_call" | custom-call | tf_op jit(solution)/shard_map/pallas_call | solution.py:755
  134.6 3.5 %reshape.7 = bf16[2,16,2,4,2560]{4,3,2,1,0:T(4,128)(2,1)} reshape(bf16[256,2560]{1,0:T(8,128)(2,1)} %shard_map.127) | data formatting | bytes 2621440 | tf_op jit(solution)/shard_map/reshape | solution.py:820

commit v4 on v3

--- a/solution.py
+++ b/solution.py
@@ -513,7 +513,7 @@
             both_ways(event, k)
     w_start(len(w_pushes))
     steps = len(early) + 1
-    w_todo = [(k + 2.5 * count, k, count) for k in range(len(pieces)) for count in range(steps)]
+    w_todo = [(k + 2 * count, k, count) for k in range(len(pieces)) for count in range(steps)]
     w_todo = [(pieces[k], count) for _, k, count in sorted(w_todo)]
 
     def core_events(e):
@@ -601,7 +601,7 @@
             arrived(a_slot(e), a_recv.at[e])
         core_events(e)
         embed_bank(far, e)
-    take_w(3)
+    take_w(2)
 
     def need_w(g):
         with jax.named_scope("need"):
@@ -696,6 +696,7 @@
             for where in blocks:
                 send_of(where, g).start()
             if g == 0 and blocks is far_blocks:
+                take_w(1)
                 for e in range(1, D):
                     embed_bank(near, e)
     keep = pltpu.make_async_copy(

time: 138 us -> 138 us (level)
  no operation moved by 1% of the time
where the time goes in v4:
time: 138 us
  Pallas kernels  135 us (98%)
  local copies, waits for them, and re-layouts  3.5 us (3%)
    pallas_call x1, Pallas kernels, body(): pl.pallas_call(functools.partial(window_kernel, (D, C, T, [x * HEAD for x...  135 us
    reshape x1, local copies, waits for them, and re-layouts, body(): return out.reshape(D, frames, height, breadth, -1)  3.5 us

profile of v4, /device:TPU:11, one launch (start us, length us, event | category | flops | bytes accessed | tf_op | source)
XLA Modules:
  0.0 138.1 jit_solution(12250715519260932093)
XLA Ops:
  0.0 134.6 %shard_map.127 = bf16[256,2560]{1,0:T(8,128)(2,1)} custom-call(bf16[320,2560]{1,0:T(8,128)(2,1)} %query_ref.1, bf16[320,2,512]{2,1,0:T(2,128)(2,1)} %keyval_ref.1, bf16[64,2560]{1,0:T(8,128)(2,1)} %in_ref.1, bf16[8,2560]{1,0:T(8,128)(2,1)} %action_ref.1, bf16[20,128]{1,0:T(8,128)(2,1)} %bitcast.4, bf16[1,16,2,4,1024]{4,3,2,1,0:T(4,128)(2,1)} %tiles_ref.1, ...), custom_call_target="tpu_custom_call" | custom-call | tf_op jit(solution)/shard_map/pallas_call | solution.py:756
  134.6 3.5 %reshape.7 = bf16[2,16,2,4,2560]{4,3,2,1,0:T(4,128)(2,1)} reshape(bf16[256,2560]{1,0:T(8,128)(2,1)} %shard_map.127) | data formatting | bytes 2621440 | tf_op jit(solution)/shard_map/reshape | solution.py:821
